TPU v7x, 32 devices: a whole 2x2x4 slice. The times are simulated.
32 devices in a mesh: rows: 16 (over z, y, x), cols: 2 (over core).
Axes of the slice: x: 2, y: 2, z: 4, core: 2. Of those that a mesh axis runs over, the one named last changes fastest.
Arguments:
- rhs: float32 [2, 96, 6144], P('cols', 'rows'), may hold values from -6 to 6
- pattern: int32 [48, 2], P(None, 'cols'), may hold values 0 or 1
- front_blocks: int32 [16, 4], replicated, may hold values from 0 to 47, as said below
- front_slot: int32 [16], replicated, may hold values from 0 to 31, as said below
- pivot_inverse: float32 [32, 256, 256], P('rows'), may hold values from -0.375 to 0.375
- update_factor: float32 [32, 256, 256], P('rows'), may hold values from -0.375 to 0.375
Outputs:
- solution: float32 [2, 96, 6144], P('cols', 'rows')
Inputs may be any that keep to these rules, and one draw needn't show every extreme that they name: `front_blocks`: columns 0 and 1 together name every row block that is no contribution block exactly once; columns 2 and 3 of a front are two different blocks, never a pivot block of any front. `front_slot`: all different; slot s belongs to index s // 2 of rows; some index holds 2 fronts in every draw; slots that no front names are unused.
All inputs are finite; a program needn't handle non-finite values. No bound on the sum of `pattern` on one device may be relied on, other than what follows from the above.
Results may differ from a plain program's by a relative error of at most 0.0001.
Values sent between devices are 32-bit elements; how exact they have to be, the bound alone decides.
A program may use at most 64 MiB of HBM per device.

v0:
```python
import jax
import jax.numpy as jnp
from jax import lax
from jax.sharding import PartitionSpec as P

BLOCK = 128
PIV = 256


def solve_slots(arrived, inverse_part, factor_part):
    width = inverse_part.shape[1]
    strict_lower = jnp.tril(jnp.ones((width, width), jnp.float32), -1)
    inverse = jnp.eye(width, dtype=jnp.float32)[None] + strict_lower[None] * inverse_part
    solved = jnp.einsum("kcj,kij->kci", arrived, inverse, precision=lax.Precision.HIGHEST)
    update = jnp.einsum("kcj,kij->kci", solved, factor_part, precision=lax.Precision.HIGHEST)
    return jnp.concatenate([solved, update], axis=2)


def on_device(rhs, pattern, front_blocks, front_slot, pivot_inverse, update_factor):
    fronts = front_blocks.shape[0]
    columns = rhs.shape[1]
    total_rows = rhs.shape[2]
    block_count = total_rows // BLOCK
    slot_dev = pivot_inverse.shape[0]
    devices = lax.axis_size("rows")
    pivot_blocks = front_blocks[:, :2].reshape(-1)
    contrib_blocks = front_blocks[:, 2:].reshape(-1)
    block_mask = pattern[:, 0].astype(jnp.float32)
    masked = rhs[0].reshape(columns, block_count, BLOCK) * block_mask[None, :, None]
    picked = jnp.swapaxes(
        jnp.take(masked, pivot_blocks, axis=1).reshape(columns, fronts, PIV), 0, 1
    )
    outbound = jnp.zeros((slot_dev * devices, columns, PIV), jnp.float32).at[front_slot].set(picked)
    arrived = lax.all_to_all(outbound, "rows", split_axis=0, concat_axis=1, tiled=True)
    worked = solve_slots(arrived, pivot_inverse, update_factor)
    returned = lax.all_to_all(worked, "rows", split_axis=1, concat_axis=0, tiled=True)
    gotten = returned[front_slot]
    solved = jnp.swapaxes(gotten[:, :, :PIV], 0, 1).reshape(columns, 2 * fronts, BLOCK)
    update = jnp.swapaxes(gotten[:, :, PIV:], 0, 1).reshape(columns, 2 * fronts, BLOCK)
    result = masked.at[:, pivot_blocks].set(solved)
    result = result.at[:, contrib_blocks].add(-update)
    return result.reshape(columns, total_rows)[None]


def solution(mesh):
    return jax.shard_map(
        on_device,
        mesh=mesh,
        in_specs=(
            P("cols", "rows", None),
            P(None, "cols"),
            P(),
            P(),
            P("rows", None, None),
            P("rows", None, None),
        ),
        out_specs=P("cols", "rows", None),
        check_vma=False,
    )
```

profile of v0, /device:TPU:0, one launch (start us, length us, event | category | flops | bytes accessed | tf_op | source)
XLA Modules:
  0.0 48.0 jit_solution(16247769093487404575)
XLA Ops:
  0.0 0.0 copy-start
  0.0 0.8 %fusion.10 = (s32[16,2]{0,1:T(2,128)S(1)}, s32[16,2]{0,1:T(2,128)S(1)}) fusion(s32[16,4]{0,1:T(4,128)} %param.8), kind=kLoop, calls=%fused_computation.31 | loop fusion | bytes 512 | tf_op jit(solution)/shard_map/slice | solution.py:27
  0.8 0.1 copy.33
  0.9 0.1 reshape.108
  1.0 0.0 copy-start.3
  1.0 0.6 %copy-done.3 = s32[48,1]{0,1:T(1,128)S(1)} copy-done((s32[48,1]{0,1:T(1,128)S(1)}, s32[48,1]{0,1:T(1,128)}, u32[]{:S(2)}) %copy-start.3) | copy-done | bytes 216
  1.7 0.1 copy.34
  1.8 0.1 broadcast_in_dim.35
  1.8 0.0 copy-start.4
  1.9 0.6 %copy-done.4 = s32[16]{0:T(128)S(1)} copy-done((s32[16]{0:T(128)S(1)}, s32[16]{0:T(128)}, u32[]{:S(2)}) %copy-start.4) | copy-done | bytes 88
  2.5 1.0 %copy_multiply_fusion = f32[6,48,128]{2,0,1:T(8,128)S(1)} fusion(f32[6,48,128]{2,1,0:T(8,128)} %bitcast.45, f32[48]{0:T(128)S(1)} %convert_bitcast_fusion), kind=kLoop, calls=%fused_computation.16 | loop fusion | flops 36864 | bytes 295104 | tf_op jit(solution)/shard_map/mul | solution.py:29
  3.5 0.6 %gather_fusion = f32[32,6,128]{2,1,0:T(8,128)S(1)} fusion(f32[6,48,128]{2,0,1:T(8,128)S(1)} %copy_multiply_fusion, s32[1024]{0:T(1024)S(1)} %pad_clamp_fusion.1), kind=kCustom, calls=%fused_computation | custom fusion | bytes 196736 | tf_op jit(solution)/shard_map/jit(_take)/gather | solution.py:31
  4.2 0.7 %broadcast_in_dim.33 = f32[32,6,256]{2,1,0:T(8,128)} broadcast(f32[]{:T(128)} %constant.10.clone.1), dimensions={} | broadcast | bytes 196612 | tf_op jit(solution)/shard_map/broadcast_in_dim | solution.py:33
  4.9 2.2 %scatter_fusion = f32[32,6,256]{2,1,0:T(8,128)} fusion(f32[32,6,256]{2,1,0:T(8,128)} %broadcast_in_dim.33, s32[16]{0:T(128)S(1)} %compare_select_fusion.2, f32[16,6,256]{2,1,0:T(8,128)S(1)} %select_bitcast_fusion), kind=kCustom, calls=%fused_computation.2 | custom fusion | bytes 294976 | tf_op jit(solution)/shard_map/scatter | solution.py:33
  7.1 8.3 %all-to-all-start = ((f32[32,6,256]{2,1,0:T(8,128)}), f32[32,6,256]{2,1,0:T(8,128)S(1)}, u32[]{:S(2)}, u32[]{:S(2)}) async-start(f32[32,6,256]{2,1,0:T(8,128)} %scatter_fusion), calls=%async_computation | async-start | bytes 524288 | tf_op jit(solution)/shard_map/all_to_all | solution.py:34
  15.4 0.0 copy-start.1
  15.5 0.1 fusion.6
  15.6 9.7 %all-to-all-done = f32[32,6,256]{2,1,0:T(8,128)S(1)} async-done(((f32[32,6,256]{2,1,0:T(8,128)}), f32[32,6,256]{2,1,0:T(8,128)S(1)}, u32[]{:S(2)}, u32[]{:S(2)}) %all-to-all-start) | async-done | bytes 196640 | tf_op jit(solution)/shard_map/all_to_all | solution.py:34
  25.3 0.1 copy.35
  25.4 0.6 %fusion = f32[2,96,256]{2,1,0:T(8,128)S(1)} fusion(f32[2,256,256]{2,1,0:T(8,128)S(1)} %copy-done.1, f32[256,256]{1,0:T(8,128)S(1)} %fusion.6, f32[256,256]{1,0:T(8,128)S(1)} %fusion.5, f32[2,96,256]{2,0,1:T(2,128)S(1)} %bitcast.41), kind=kOutput, calls=%fused_computation.5 | convolution fusion | flops 151257088 | bytes 1441792 | tf_op jit(solution)/shard_map/kcj,kij->kci/dot_general | solution.py:14
  26.1 0.0 copy-done
  26.1 0.6 %fusion.11 = f32[2,96,256]{2,1,0:T(8,128)S(1)} fusion(f32[2,96,256]{2,1,0:T(8,128)S(1)} %fusion, f32[2,256,256]{2,1,0:T(8,128)S(1)} %copy-done), kind=kOutput, calls=%fused_computation.32 | convolution fusion | flops 150994944 | bytes 917504 | tf_op jit(solution)/shard_map/kcj,kij->kci/dot_general | solution.py:15
  26.7 1.1 %copy.37 = f32[2,96,512]{2,0,1:T(2,128)} copy(f32[2,96,512]{2,1,0:T(8,128)S(1)} %pad_maximum_fusion) | data formatting | bytes 786432 | tf_op jit(solution)/shard_map/concatenate | solution.py:16
  27.8 3.6 %all-to-all-start.1 = ((f32[2,96,512]{2,0,1:T(2,128)}), f32[2,96,512]{2,0,1:T(2,128)S(1)}, u32[]{:S(2)}, u32[]{:S(2)}) async-start(f32[2,96,512]{2,0,1:T(2,128)} %copy.37), calls=%async_computation.1 | async-start | bytes 786432 | tf_op jit(solution)/shard_map/all_to_all | solution.py:36
  31.3 0.1 copy.40
  31.4 0.1 reshape.110
  31.5 11.8 %all-to-all-done.1 = f32[2,96,512]{2,0,1:T(2,128)S(1)} async-done(((f32[2,96,512]{2,0,1:T(2,128)}), f32[2,96,512]{2,0,1:T(2,128)S(1)}, u32[]{:S(2)}, u32[]{:S(2)}) %all-to-all-start.1) | async-done | bytes 393248 | tf_op jit(solution)/shard_map/all_to_all | solution.py:36
  43.3 0.1 copy.42
  43.4 0.6 %gather_fusion.1 = f32[16,6,512]{2,1,0:T(8,128)S(1)} fusion(f32[32,6,512]{2,1,0:T(8,128)S(1)} %bitcast.39, s32[1024]{0:T(1024)S(1)} %pad_clamp_fusion), kind=kCustom, calls=%fused_computation.1 | custom fusion | bytes 393280 | tf_op jit(solution)/shard_map/gather | solution.py:37
  44.0 1.5 %scatter_fusion.1 = f32[6,48,128]{2,0,1:T(8,128)S(1)} fusion(f32[6,48,128]{2,0,1:T(8,128)S(1)} %copy_multiply_fusion, s32[32]{0:T(128)S(1)} %fusion.8, f32[32,6,128]{2,1,0:T(8,128)S(1)} %bitcast.44), kind=kCustom, calls=%fused_computation.3 | custom fusion | bytes 295040 | tf_op jit(solution)/shard_map/scatter | solution.py:40
  45.5 1.7 %scatter_fusion.2 = f32[6,48,128]{2,0,1:T(8,128)S(1)} fusion(f32[6,48,128]{2,0,1:T(8,128)S(1)} %scatter_fusion.1, s32[32]{0:T(128)S(1)} %fusion.9, f32[32,6,128]{2,1,0:T(8,128)S(1)} %bitcast.43), kind=kCustom, calls=%fused_computation.4 | custom fusion | flops 24576 | bytes 295040 | tf_op jit(solution)/shard_map/scatter-add | solution.py:41
  47.2 0.8 %copy.41 = f32[1,6,6144]{2,0,1:T(1,128)} copy(f32[1,6,6144]{2,1,0:T(8,128)S(1)} %bitcast.37) | data formatting | bytes 294912 | tf_op jit(solution)/shard_map/broadcast_in_dim;reshape | solution.py:42
  (16 shorter events, 0.2 us)
Async XLA Ops:
  0.0 26.1 %copy-start = (f32[2,256,256]{2,1,0:T(8,128)S(1)}, f32[2,256,256]{2,1,0:T(8,128)}, u32[]{:S(2)}) copy-start(f32[2,256,256]{2,1,0:T(8,128)} %param.11) | copy-start | bytes 1572868
  0.0 0.8 %copy-start.2 = (s32[16,4]{0,1:T(4,128)S(1)}, s32[16,4]{0,1:T(4,128)}, u32[]{:S(2)}) copy-start(s32[16,4]{0,1:T(4,128)} %param.8) | copy-start | bytes 772
  1.0 0.7 %copy-start.3 = (s32[48,1]{0,1:T(1,128)S(1)}, s32[48,1]{0,1:T(1,128)}, u32[]{:S(2)}) copy-start(s32[48,1]{0,1:T(1,128)} %param.7) | copy-start | bytes 580
  1.8 0.7 %copy-start.4 = (s32[16]{0:T(128)S(1)}, s32[16]{0:T(128)}, u32[]{:S(2)}) copy-start(s32[16]{0:T(128)} %param.9) | copy-start | bytes 196
  7.1 18.2 %all-to-all-start = ((f32[32,6,256]{2,1,0:T(8,128)}), f32[32,6,256]{2,1,0:T(8,128)S(1)}, u32[]{:S(2)}, u32[]{:S(2)}) async-start(f32[32,6,256]{2,1,0:T(8,128)} %scatter_fusion), calls=%async_computation | async-start | bytes 524288 | tf_op jit(solution)/shard_map/all_to_all | solution.py:34
  15.4 10.0 %copy-start.1 = (f32[2,256,256]{2,1,0:T(8,128)S(1)}, f32[2,256,256]{2,1,0:T(8,128)}, u32[]{:S(2)}) copy-start(f32[2,256,256]{2,1,0:T(8,128)} %param.10) | copy-start | bytes 1572868
  27.8 15.5 %all-to-all-start.1 = ((f32[2,96,512]{2,0,1:T(2,128)}), f32[2,96,512]{2,0,1:T(2,128)S(1)}, u32[]{:S(2)}, u32[]{:S(2)}) async-start(f32[2,96,512]{2,0,1:T(2,128)} %copy.37), calls=%async_computation.1 | async-start | bytes 786432 | tf_op jit(solution)/shard_map/all_to_all | solution.py:36
where the time goes:
time: 48.4 us; the launch traced here: 48 us
  waiting for transfers between devices  21.5 us (44%)
  starting transfers between devices  11.9 us (25%)
  local copies, waits for them, and re-layouts  10.2 us (21%)
  other arithmetic  2.92 us (6%)
  matrix products  1.25 us (3%)
    all_to_all x1, waiting for transfers between devices, on_device(): lax.all_to_all(worked, 'rows', split_axis=1, concat_axis=0, tiled=True)  11.8 us
    all_to_all x1, waiting for transfers between devices, on_device(): lax.all_to_all(outbound, 'rows', split_axis=0, concat_axis=1, tiled=True)  9.71 us
    all_to_all x1, starting transfers between devices, on_device(): lax.all_to_all(outbound, 'rows', split_axis=0, concat_axis=1, tiled=True)  8.34 us
    all_to_all x1, starting transfers between devices, on_device(): lax.all_to_all(worked, 'rows', split_axis=1, concat_axis=0, tiled=True)  3.56 us
    scatter x1, local copies, waits for them, and re-layouts, on_device(): jnp.zeros((slot_dev * devices, columns, PIV), jnp.float32).at[front_slot]  2.2 us
    scatter-add x1, other arithmetic, on_device(): result = result.at[:, contrib_blocks].add(-update)  1.66 us
    scatter x1, local copies, waits for them, and re-layouts, on_device(): result = masked.at[:, pivot_blocks].set(solved)  1.48 us
    unnamed x11, local copies, waits for them, and re-layouts  1.3 us
  transfers between devices with their start and end apart: 2, of which 2 were waited for; matrix products, arithmetic and copies ran while one was open for 1% of the time, Pallas kernels for 0%

commit v1 on v0

--- a/solution.py
+++ b/solution.py
@@ -31,7 +31,10 @@
         jnp.take(masked, pivot_blocks, axis=1).reshape(columns, fronts, PIV), 0, 1
     )
     outbound = jnp.zeros((slot_dev * devices, columns, PIV), jnp.float32).at[front_slot].set(picked)
-    arrived = lax.all_to_all(outbound, "rows", split_axis=0, concat_axis=1, tiled=True)
+    arrived = jnp.concatenate(
+        lax.all_to_all(jnp.stack(jnp.split(outbound, lax.axis_size("rows"), axis=0)), "rows", 0, 0),
+        axis=1,
+    )
     worked = solve_slots(arrived, pivot_inverse, update_factor)
     returned = lax.all_to_all(worked, "rows", split_axis=1, concat_axis=0, tiled=True)
     gotten = returned[front_slot]

time: 48.4 us -> 46.3 us (0.957)
  waiting for transfers between devices: 21.5 us -> 20.3 us
  local copies, waits for them, and re-layouts: 10.2 us -> 9.09 us
    all_to_all x1, waiting for transfers between devices: 9.71 us -> 8.5 us  [on_device(): lax.all_to_all(jnp.stack(jnp.split(outbound, lax.axis_size('rows'), axis=...]
    scatter x1, local copies, waits for them, and re-layouts: 2.2 us -> 1.02 us  [on_device(): jnp.zeros((slot_dev * devices, columns, PIV), jnp.float32).at[front_slot]]
    another operation x0 -> x2, local copies, waits for them, and re-layouts: none -> 0.78 us  [on_device(): jnp.stack(jnp.split(outbound, lax.axis_size('rows'), axis=0))]
    broadcast_in_dim x1, local copies, waits for them, and re-layouts: 0.71 us -> 0.02 us  [on_device(): jnp.zeros((slot_dev * devices, columns, PIV), jnp.float32).at[front_slot]]
    unnamed x11 -> x26, local copies, waits for them, and re-layouts: 1.3 us -> 1.36 us
where the time goes in v1:
time: 46.3 us; the launch traced here: 45.9 us
  waiting for transfers between devices  20.3 us (44%)
  starting transfers between devices  12 us (26%)
  local copies, waits for them, and re-layouts  9.09 us (20%)
  other arithmetic  2.92 us (6%)
  matrix products  1.25 us (3%)
    all_to_all x1, waiting for transfers between devices, on_device(): lax.all_to_all(worked, 'rows', split_axis=1, concat_axis=0, tiled=True)  11.8 us
    all_to_all x1, waiting for transfers between devices, on_device(): lax.all_to_all(jnp.stack(jnp.split(outbound, lax.axis_size('rows'), axis=...  8.5 us
    all_to_all x1, starting transfers between devices, on_device(): lax.all_to_all(jnp.stack(jnp.split(outbound, lax.axis_size('rows'), axis=...  8.47 us
    all_to_all x1, starting transfers between devices, on_device(): lax.all_to_all(worked, 'rows', split_axis=1, concat_axis=0, tiled=True)  3.55 us
    scatter-add x1, other arithmetic, on_device(): result = result.at[:, contrib_blocks].add(-update)  1.66 us
    scatter x1, local copies, waits for them, and re-layouts, on_device(): result = masked.at[:, pivot_blocks].set(solved)  1.48 us
    unnamed x26, local copies, waits for them, and re-layouts  1.36 us
    concatenate x1, local copies, waits for them, and re-layouts, solve_slots(): return jnp.concatenate([solved, update], axis=2)  1.05 us
  transfers between devices with their start and end apart: 2, of which 2 were waited for; matrix products, arithmetic and copies ran while one was open for 1% of the time, Pallas kernels for 0%

profile of v1, /device:TPU:0, one launch (start us, length us, event | category | flops | bytes accessed | tf_op | source)
XLA Modules:
  0.0 45.9 jit_solution(15450669834033965355)
XLA Ops:
  0.0 0.0 copy-start
  0.0 0.0 copy-start.2
  0.0 0.8 %fusion.10 = (s32[16,2]{0,1:T(2,128)S(1)}, s32[16,2]{0,1:T(2,128)S(1)}) fusion(s32[16,4]{0,1:T(4,128)} %param.8), kind=kLoop, calls=%fused_computation.63 | loop fusion | bytes 512 | tf_op jit(solution)/shard_map/slice | solution.py:27
  0.8 0.0 copy-done.2
  0.8 0.1 copy.33
  0.9 0.1 reshape.114
  1.0 0.0 copy-start.3
  1.0 0.6 %copy-done.3 = s32[16]{0:T(128)S(1)} copy-done((s32[16]{0:T(128)S(1)}, s32[16]{0:T(128)}, u32[]{:S(2)}) %copy-start.3) | copy-done | bytes 88
  1.6 0.6 %copy-done.4 = s32[48,1]{0,1:T(1,128)S(1)} copy-done((s32[48,1]{0,1:T(1,128)S(1)}, s32[48,1]{0,1:T(1,128)}, u32[]{:S(2)}) %copy-start.4) | copy-done | bytes 216
  2.3 0.1 copy.34
  2.4 0.1 broadcast_in_dim.35
  2.5 1.0 %copy_multiply_fusion = f32[6,48,128]{2,0,1:T(8,128)S(1)} fusion(f32[6,48,128]{2,1,0:T(8,128)} %bitcast.107, f32[48]{0:T(128)S(1)} %convert_bitcast_fusion), kind=kLoop, calls=%fused_computation.16 | loop fusion | flops 36864 | bytes 295104 | tf_op jit(solution)/shard_map/mul | solution.py:29
  3.5 0.6 %gather_fusion = f32[32,6,128]{2,1,0:T(8,128)S(1)} fusion(f32[6,48,128]{2,0,1:T(8,128)S(1)} %copy_multiply_fusion, s32[1024]{0:T(1024)S(1)} %get-tuple-element.10), kind=kCustom, calls=%fused_computation | custom fusion | bytes 196736 | tf_op jit(solution)/shard_map/jit(_take)/gather | solution.py:31
  4.2 1.0 %scatter_fusion = f32[32,6,256]{2,1,0:T(8,128)S(1)} fusion(f32[32,6,256]{2,1,0:T(8,128)S(1)} %broadcast_in_dim.33, s32[16]{0:T(128)S(1)} %compare_select_fusion.2, f32[16,6,256]{2,1,0:T(8,128)S(1)} %select_bitcast_fusion), kind=kCustom, calls=%fused_computation.2 | custom fusion | bytes 294976 | tf_op jit(solution)/shard_map/scatter | solution.py:33
  5.4 0.8 %copy.35 = f32[16,2,6,256]{3,1,2,0:T(2,128)} copy(f32[16,2,6,256]{3,2,1,0:T(8,128)S(1)} %constant_dynamic-update-slice_fusion) | data formatting | bytes 393216 | tf_op jit(solution)/shard_map/stack | solution.py:35
  6.2 8.5 %all-to-all-start = ((f32[16,2,6,256]{3,1,2,0:T(2,128)}), f32[16,2,6,256]{3,1,2,0:T(2,128)S(1)}, u32[]{:S(2)}, u32[]{:S(2)}) async-start(f32[16,2,6,256]{3,1,2,0:T(2,128)} %copy.35), calls=%async_computation | async-start | bytes 393216 | tf_op jit(solution)/shard_map/all_to_all | solution.py:35
  14.7 0.1 fusion.6
  14.8 8.5 %all-to-all-done = f32[16,2,6,256]{3,1,2,0:T(2,128)S(1)} async-done(((f32[16,2,6,256]{3,1,2,0:T(2,128)}), f32[16,2,6,256]{3,1,2,0:T(2,128)S(1)}, u32[]{:S(2)}, u32[]{:S(2)}) %all-to-all-start) | async-done | bytes 196640 | tf_op jit(solution)/shard_map/all_to_all | solution.py:35
  23.3 0.0 copy-done.1
  23.3 0.6 %fusion = f32[2,96,256]{2,1,0:T(8,128)S(1)} fusion(f32[2,256,256]{2,1,0:T(8,128)S(1)} %copy-done.1, f32[256,256]{1,0:T(8,128)S(1)} %fusion.6, f32[256,256]{1,0:T(8,128)S(1)} %fusion.5, f32[2,96,256]{2,0,1:T(2,128)S(1)} %bitcast.103), kind=kOutput, calls=%fused_computation.5 | convolution fusion | flops 151257088 | bytes 1441792 | tf_op jit(solution)/shard_map/kcj,kij->kci/dot_general | solution.py:14
  24.0 0.0 copy-done
  24.0 0.6 %fusion.11 = f32[2,96,256]{2,1,0:T(8,128)S(1)} fusion(f32[2,96,256]{2,1,0:T(8,128)S(1)} %fusion, f32[2,256,256]{2,1,0:T(8,128)S(1)} %copy-done), kind=kOutput, calls=%fused_computation.64 | convolution fusion | flops 150994944 | bytes 917504 | tf_op jit(solution)/shard_map/kcj,kij->kci/dot_general | solution.py:15
  24.6 1.1 %copy.37 = f32[2,96,512]{2,0,1:T(2,128)} copy(f32[2,96,512]{2,1,0:T(8,128)S(1)} %pad_maximum_fusion) | data formatting | bytes 786432 | tf_op jit(solution)/shard_map/concatenate | solution.py:16
  25.7 3.6 %all-to-all-start.1 = ((f32[2,96,512]{2,0,1:T(2,128)}), f32[2,96,512]{2,0,1:T(2,128)S(1)}, u32[]{:S(2)}, u32[]{:S(2)}) async-start(f32[2,96,512]{2,0,1:T(2,128)} %copy.37), calls=%async_computation.1 | async-start | bytes 786432 | tf_op jit(solution)/shard_map/all_to_all | solution.py:39
  29.2 0.1 copy.40
  29.3 0.1 reshape.118
  29.4 11.8 %all-to-all-done.1 = f32[2,96,512]{2,0,1:T(2,128)S(1)} async-done(((f32[2,96,512]{2,0,1:T(2,128)}), f32[2,96,512]{2,0,1:T(2,128)S(1)}, u32[]{:S(2)}, u32[]{:S(2)}) %all-to-all-start.1) | async-done | bytes 393248 | tf_op jit(solution)/shard_map/all_to_all | solution.py:39
  41.3 0.1 copy.42
  41.4 0.6 %gather_fusion.1 = f32[16,6,512]{2,1,0:T(8,128)S(1)} fusion(f32[32,6,512]{2,1,0:T(8,128)S(1)} %bitcast.102, s32[1024]{0:T(1024)S(1)} %get-tuple-element.9), kind=kCustom, calls=%fused_computation.1 | custom fusion | bytes 393280 | tf_op jit(solution)/shard_map/gather | solution.py:40
  42.0 1.5 %scatter_fusion.1 = f32[6,48,128]{2,0,1:T(8,128)S(1)} fusion(f32[6,48,128]{2,0,1:T(8,128)S(1)} %copy_multiply_fusion, s32[32]{0:T(128)S(1)} %fusion.8, f32[32,6,128]{2,1,0:T(8,128)S(1)} %bitcast.106), kind=kCustom, calls=%fused_computation.3 | custom fusion | bytes 295040 | tf_op jit(solution)/shard_map/scatter | solution.py:43
  43.5 1.7 %scatter_fusion.2 = f32[6,48,128]{2,0,1:T(8,128)S(1)} fusion(f32[6,48,128]{2,0,1:T(8,128)S(1)} %scatter_fusion.1, s32[32]{0:T(128)S(1)} %fusion.9, f32[32,6,128]{2,1,0:T(8,128)S(1)} %bitcast.105), kind=kCustom, calls=%fused_computation.4 | custom fusion | flops 24576 | bytes 295040 | tf_op jit(solution)/shard_map/scatter-add | solution.py:44
  45.1 0.8 %copy.41 = f32[1,6,6144]{2,0,1:T(1,128)} copy(f32[1,6,6144]{2,1,0:T(8,128)S(1)} %bitcast.100) | data formatting | bytes 294912 | tf_op jit(solution)/shard_map/broadcast_in_dim;reshape | solution.py:45
  (31 shorter events, 0.2 us)
Async XLA Ops:
  0.0 24.0 %copy-start = (f32[2,256,256]{2,1,0:T(8,128)S(1)}, f32[2,256,256]{2,1,0:T(8,128)}, u32[]{:S(2)}) copy-start(f32[2,256,256]{2,1,0:T(8,128)} %param.11) | copy-start | bytes 1572868
  0.0 0.8 %copy-start.2 = (s32[16,4]{0,1:T(4,128)S(1)}, s32[16,4]{0,1:T(4,128)}, u32[]{:S(2)}) copy-start(s32[16,4]{0,1:T(4,128)} %param.8) | copy-start | bytes 772
  1.0 0.7 %copy-start.3 = (s32[16]{0:T(128)S(1)}, s32[16]{0:T(128)}, u32[]{:S(2)}) copy-start(s32[16]{0:T(128)} %param.9) | copy-start | bytes 196
  1.6 0.7 %copy-start.4 = (s32[48,1]{0,1:T(1,128)S(1)}, s32[48,1]{0,1:T(1,128)}, u32[]{:S(2)}) copy-start(s32[48,1]{0,1:T(1,128)} %param.7) | copy-start | bytes 580
  6.2 17.1 %copy-start.1 = (f32[2,256,256]{2,1,0:T(8,128)S(1)}, f32[2,256,256]{2,1,0:T(8,128)}, u32[]{:S(2)}) copy-start(f32[2,256,256]{2,1,0:T(8,128)} %param.10) | copy-start | bytes 1572868
  6.2 17.1 %all-to-all-start = ((f32[16,2,6,256]{3,1,2,0:T(2,128)}), f32[16,2,6,256]{3,1,2,0:T(2,128)S(1)}, u32[]{:S(2)}, u32[]{:S(2)}) async-start(f32[16,2,6,256]{3,1,2,0:T(2,128)} %copy.35), calls=%async_computation | async-start | bytes 393216 | tf_op jit(solution)/shard_map/all_to_all | solution.py:35
  25.7 15.6 %all-to-all-start.1 = ((f32[2,96,512]{2,0,1:T(2,128)}), f32[2,96,512]{2,0,1:T(2,128)S(1)}, u32[]{:S(2)}, u32[]{:S(2)}) async-start(f32[2,96,512]{2,0,1:T(2,128)} %copy.37), calls=%async_computation.1 | async-start | bytes 786432 | tf_op jit(solution)/shard_map/all_to_all | solution.py:39
